TPU v7x, 32 devices: a 4x4x1 block of a 4x4x8 slice. The times are simulated.
32 devices in a mesh: dp: 1 (over z), tp: 4 (over y), ep: 8 (over x, core).
Axes of the slice: x: 4, y: 4, z: 1, core: 2. Of those that a mesh axis runs over, the one named last changes fastest.
The devices are a block of a 4x4x8 slice.
Arguments:
- x: bfloat16 [2048, 2048], P(('dp', 'ep', 'tp'))
- idx: int32 [2048, 6], P(('dp', 'ep', 'tp'))
- gate: float32 [2048, 6], P(('dp', 'ep', 'tp'))
- w1: bfloat16 [64, 2048, 1408], P('ep', None, 'tp')
- w3: bfloat16 [64, 2048, 1408], P('ep', None, 'tp')
- w2: bfloat16 [64, 1408, 2048], P('ep', 'tp')
Outputs:
- output: bfloat16 [2048, 2048], P(('dp', 'ep', 'tp'))
All inputs are finite; a program needn't handle non-finite values.
Results may differ from a plain program's by a relative error of at most 0.001.
Values are sent between devices in bfloat16 or wider.
A program may use at most 768 MiB of HBM per device.

v0:
```python
import jax
import jax.numpy as jnp
from jax import lax
from jax.sharding import PartitionSpec as P


def _groups(idx, gate, lo, n_exp, cap):
    k = idx.shape[1]
    flat = idx.reshape(-1) - lo
    key = jnp.where((flat >= 0) & (flat < n_exp), flat, n_exp)
    order = jnp.argsort(key)
    counts = jnp.zeros((n_exp + 1,), jnp.int32).at[key].add(1)[:n_exp]
    starts = jnp.cumsum(counts) - counts
    slot = jnp.arange(cap)
    pid = order[jnp.clip(starts[:, None] + slot[None, :], 0, flat.shape[0] - 1)]
    g = jnp.where(slot[None, :] < counts[:, None], gate.reshape(-1)[pid], 0.0)
    return pid // k, g


def _experts(x, tok, g, w1, w3, w2):
    xg = x[tok]
    a = jnp.einsum('ecd,edf->ecf', xg, w1, preferred_element_type=jnp.float32)
    b = jnp.einsum('ecd,edf->ecf', xg, w3, preferred_element_type=jnp.float32)
    h = (jax.nn.silu(a) * b).astype(jnp.bfloat16)
    o = jnp.einsum('ecf,efd->ecd', h, w2, preferred_element_type=jnp.float32) * g[..., None]
    d = x.shape[1]
    return jnp.zeros(x.shape, jnp.float32).at[tok.reshape(-1)].add(o.reshape(-1, d))


def solution(mesh):
    n_pos = mesh.shape['ep']
    rows_spec = P(('dp', 'ep', 'tp'), None)

    def body(x, idx, gate, w1, w3, w2):
        xa = lax.all_gather(x, ('ep', 'tp'), axis=0, tiled=True)
        ia = lax.all_gather(idx, ('ep', 'tp'), axis=0, tiled=True)
        ga = lax.all_gather(gate, ('ep', 'tp'), axis=0, tiled=True)
        rows = xa.shape[0]
        n_exp, k = w1.shape[0], idx.shape[1]
        cap = 8 * ((k * rows // (n_exp * n_pos) + 9) // 8)
        lo = lax.axis_index('ep') * n_exp
        tok, g = _groups(ia, ga, lo, n_exp, cap)
        part = _experts(xa, tok, g, w1, w3, w2)
        y = lax.psum_scatter(part, ('ep', 'tp'), scatter_dimension=0, tiled=True)
        return y.astype(jnp.bfloat16)

    return jax.shard_map(body, mesh=mesh,
                         in_specs=(rows_spec, rows_spec, rows_spec,
                                   P('ep', None, 'tp'), P('ep', None, 'tp'), P('ep', 'tp', None)),
                         out_specs=rows_spec, check_vma=False)
```

profile of v0, /device:TPU:97, one launch (start us, length us, event | category | flops | bytes accessed | tf_op | source)
XLA Modules:
  0.0 398.5 jit_solution(14182540355987933429)
XLA Ops:
  6.5 0.0 all-gather.4.cloned.1.call-start
  6.6 0.7 all-gather.4.cloned.1.call-update
  7.3 0.1 reduce-scatter.2.cloned.1.call-start
  7.4 32.5 %all-gather = s32[32,64,6]{1,2,0:T(8,128)S(1)} all-gather(s32[1,64,6]{1,2,0:T(8,128)} %bitcast.32), channel_id=1, replica_groups=mesh['dp'=1,'tp'=4,'ep'=8] {'ep','tp'}, dimensions={0}, use_global_device_ids=true | all-gather | bytes 50688 | tf_op jit(solution)/shard_map/all_gather | solution.py:36
  39.9 0.4 copy.14
  40.3 0.8 sub.33
  41.1 0.7 sub.32
  41.8 33.1 %all-gather.1 = f32[32,64,6]{1,2,0:T(8,128)S(1)} all-gather(f32[1,64,6]{1,2,0:T(8,128)} %bitcast.33), channel_id=1, replica_groups=mesh['dp'=1,'tp'=4,'ep'=8] {'ep','tp'}, dimensions={0}, use_global_device_ids=true | all-gather | bytes 50688 | tf_op jit(solution)/shard_map/all_gather | solution.py:37
  74.9 0.4 copy.16
  75.3 0.7 reshape.251
  76.0 0.1 compare_select_fusion
  76.1 97.2 %scatter_custom_fusion = s32[9]{0:T(128)S(1)} fusion(s32[12288]{0:T(1024)S(1)} %bitcast.31, s32[12288]{0:T(1024)S(1)} %broadcast.266, s32[]{:T(128)} %constant.15.clone.1), kind=kCustom, calls=%fused_computation.33 | custom fusion | flops 12288 | bytes 40 | tf_op jit(solution)/shard_map/scatter-add | solution.py:12
  173.3 0.2 reduce-window.9
  173.5 0.1 compare_select_fusion.4
  173.6 0.1 reshape.255
  173.7 8.2 %sort.17 = (s32[12288]{0:T(1024)}, s32[12288]{0:T(1024)S(1)}) sort(s32[12288]{0:T(1024)S(1)} %and_select_fusion.1, s32[12288]{0:T(1024)S(1)} %iota.14), dimensions={0}, to_apply=%region_0.1 | sort | flops 172032 | bytes 196608 | tf_op jit(solution)/shard_map/jit(argsort)/sort | solution.py:11
  181.9 8.8 %gather_fusion = s32[1600]{0:T(1024)S(1)} fusion(s32[12288]{0:T(1024)S(1)} %get-tuple-element.6, s32[2048]{0:T(1024)S(1)} %pad_clamp_fusion.2), kind=kCustom, calls=%fused_computation | custom fusion | bytes 19200 | tf_op jit(solution)/shard_map/gather | solution.py:15
  190.7 0.1 gather.12
  190.8 0.1 reshape.263
  190.9 0.1 reshape.271
  191.0 8.8 %gather_fusion.2 = f32[1600]{0:T(1024)S(1)} fusion(f32[12288]{0:T(1024)S(1)} %reshape.251, s32[2048]{0:T(1024)S(1)} %pad_clamp_fusion), kind=kCustom, calls=%fused_computation.2 | custom fusion | bytes 19200 | tf_op jit(solution)/shard_map/gather | solution.py:16
  199.8 0.1 reshape.270
  199.9 0.1 fusion.3
  200.0 0.0 all-gather.4.cloned.1.call-done
  200.0 18.8 %gather_fusion.1 = bf16[1600,2048]{1,0:T(8,128)(2,1)} fusion(bf16[2048,2048]{1,0:T(8,128)(2,1)} %all-gather.4.cloned.1.call-done, s32[2048]{0:T(1024)S(1)} %pad_clamp_fusion.1), kind=kCustom, calls=%fused_computation.1 | custom fusion | bytes 13113600 | tf_op jit(solution)/shard_map/gather | solution.py:21
  218.8 10.3 %fusion.9 = f32[8,200,352]{2,1,0:T(8,128)S(1)} fusion(bf16[8,200,2048]{2,1,0:T(8,128)(2,1)} %bitcast.29, bf16[8,2048,352]{1,2,0:T(8,128)(2,1)} %param.9), kind=kOutput, calls=%fused_computation.37 | convolution fusion | flops 2306867200 | bytes 20340736 | tf_op jit(solution)/shard_map/ecd,edf->ecf/dot_general | solution.py:22
  229.1 16.1 %broadcast_multiply_fusion = f32[8,200,2048]{2,1,0:T(8,128)} fusion(f32[8,200]{1,0:T(8,128)S(1)} %fusion.3, bf16[8,352,2048]{2,1,0:T(8,128)(2,1)} %param.11, f32[8,200,352]{2,1,0:T(8,128)S(1)} %fusion.9, bf16[8,200,2048]{2,1,0:T(8,128)(2,1)} %bitcast.30, bf16[8,2048,352]{1,2,0:T(8,128)(2,1)} %param.10), kind=kOutput, calls=%fused_computation.7 | convolution fusion | flops 4620390400 | bytes 44988672 | tf_op jit(solution)/shard_map/ecf,efd->ecd/dot_general | solution.py:25
  245.2 33.9 %scatter_custom_fusion.1 = f32[2048,2048]{1,0:T(8,128)} fusion(s32[1600]{0:T(1024)S(1)} %fusion.5, f32[1600,2048]{1,0:T(8,128)} %bitcast.34, f32[]{:T(128)} %constant.12.clone.1), kind=kCustom, calls=%fused_computation.5 | custom fusion | flops 3276800 | bytes 16777728 | tf_op jit(solution)/shard_map/scatter-add | solution.py:27
  279.1 0.1 reduce-scatter.2.cloned.1.call-update
  279.2 110.3 %reduce-scatter.2.cloned.1.call-done = f32[64,2048]{1,0:T(8,128)} async-done(((f32[2048,2048]{1,0:T(8,128)}), f32[64,2048]{1,0:T(8,128)}) %reduce-scatter.2.cloned.1.call-update) | async-done | bytes 524304 | tf_op jit(solution)/shard_map/reduce_scatter | solution.py:44
  389.5 1.8 convert_element_type.7
  (13 shorter events, 0.1 us)
Async XLA Ops:
  6.5 193.5 %all-gather.4.cloned.1.call-start = ((), (), s32[]{:S(2)}) async-start(), calls=%async_computation.1 | async-start | bytes 8650752 | tf_op jit(solution)/shard_map/all_gather | solution.py:35
  7.3 382.2 %reduce-scatter.2.cloned.1.call-start = ((), (), s32[]{:S(2)}) async-start(), calls=%async_computation.2 | async-start | bytes 17301504 | tf_op jit(solution)/shard_map/reduce_scatter | solution.py:44
Sparse Core Ops, SparseCore 0:
  9.4 51.9 all-gather.3
  279.3 110.1 reduce-scatter.1
where the time goes:
time: 400 us; the launch traced here: 398 us
  other arithmetic  142 us (36%)
  waiting for transfers between devices  111 us (28%)
  blocking collectives  65.6 us (16%)
  local copies, waits for them, and re-layouts  39.8 us (10%)
  matrix products  26.4 us (7%)
  between operations  14 us (4%)
    reduce_scatter x1, waiting for transfers between devices, body(): y = lax.psum_scatter(part, ('ep', 'tp'), scatter_dimension=0, tiled=True)  110 us
    scatter-add x1, other arithmetic, _groups(): counts = jnp.zeros((n_exp + 1,), jnp.int32).at[key].add(1)[:n_exp]  97.2 us
    scatter-add x1, other arithmetic, _experts(): jnp.zeros(x.shape, jnp.float32).at[tok.reshape(-1)].add(o.reshape(-1, d))  33.9 us
    all_gather x1, blocking collectives, body(): ga = lax.all_gather(gate, ('ep', 'tp'), axis=0, tiled=True)  33.1 us
    all_gather x1, blocking collectives, body(): ia = lax.all_gather(idx, ('ep', 'tp'), axis=0, tiled=True)  32.5 us
    gather x1, local copies, waits for them, and re-layouts, _experts(): xg = x[tok]  18.8 us
    dot_general x1, matrix products, _experts(): jnp.einsum('ecf,efd->ecd', h, w2, preferred_element_type=jnp.float32)  16.1 us
    dot_general x1, matrix products, _experts(): a = jnp.einsum('ecd,edf->ecf', xg, w1, preferred_element_type=jnp.float32)  10.3 us
  transfers between devices with their start and end apart: 2, of which 1 were waited for; matrix products, arithmetic and copies ran while one was open for 32% of the time, Pallas kernels for 0%

commit v1 on v0

v1 whole, which is shorter than its diff:
```python
import functools

import jax
import jax.numpy as jnp
from jax import lax
from jax.experimental import pallas as pl
from jax.experimental.pallas import tpu as pltpu
from jax.sharding import PartitionSpec as P

MESH = pl.DeviceIdType.MESH
F32, BF16 = jnp.float32, jnp.bfloat16
META = 128
COLS = 512


def _kernel(n_ep, x_ref, idx_ref, gate_ref, w1_hbm, w3_hbm, w2_hbm, y_ref,
            st, send, xr, w1, w3, w2, hid, gat, part, near, full, back,
            w_sem, xs, xv, ys, yv, fs, fv, ns, nv, us, uv, bs, bv):
    rows, width = x_ref.shape
    top = idx_ref.shape[1]
    n_exp = w1.shape[0]
    blk = 2 * rows // n_ep
    half_ep = n_ep // 2
    kl_n = n_ep // 2
    via = kl_n // 2
    vrows = kl_n * blk
    crows = 4 * vrows
    n_col = width // COLS

    p, t = lax.axis_index('ep'), lax.axis_index('tp')
    cx, cc = p // 2, p % 2
    up, dn = {'tp': (t + 1) % 4}, {'tp': (t + 3) % 4}

    def dest(k):
        return {'ep': 2 * ((cx + half_ep - k // 2) % half_ep) + (cc + k % 2) % 2}

    def home(k):
        return {'ep': 2 * ((cx + k // 2) % half_ep) + (cc + k % 2) % 2}

    def place(k, v):
        return pl.ds((k // kl_n) * crows + v * vrows + (k % kl_n) * blk, blk)

    def remote(src, dst, s, r, dev):
        return pltpu.make_async_remote_copy(src_ref=src, dst_ref=dst, send_sem=s, recv_sem=r,
                                            device_id=dev, device_id_type=MESH)

    def weights(e):
        return [pltpu.make_async_copy(h.at[e], v.at[e], w_sem.at[i, e])
                for i, (h, v) in enumerate(((w1_hbm, w1), (w3_hbm, w3), (w2_hbm, w2)))]

    for e in range(n_exp):
        for c in weights(e)[:2]:
            c.start()
    for e in range(n_exp):
        weights(e)[2].start()

    barrier = pltpu.get_barrier_semaphore()
    for k in range(1, n_ep):
        pl.semaphore_signal(barrier, inc=1, device_id=dest(k), device_id_type=MESH)
    pl.semaphore_signal(barrier, inc=1, device_id=up, device_id_type=MESH)
    pl.semaphore_signal(barrier, inc=1, device_id=dn, device_id_type=MESH)

    idx = idx_ref[...]
    gate = gate_ref[...]
    lanes = n_ep * blk
    lane = lax.broadcasted_iota(jnp.int32, (rows, lanes), 1)
    kk = lax.div(lane, blk)
    pos_of = 2 * lax.rem(cx + half_ep - lax.div(kk, 2), half_ep) + lax.rem(cc + lax.rem(kk, 2), 2)
    first = pos_of * n_exp
    hit = jnp.zeros((rows, lanes), F32)
    for j in range(top):
        col = idx[:, j:j + 1]
        hit = jnp.where((col >= first) & (col < first + n_exp), 1.0, hit)
    lower = jnp.where(lax.broadcasted_iota(jnp.int32, (rows, rows), 0) > lax.broadcasted_iota(jnp.int32, (rows, rows), 1),
                      1.0, 0.0)
    rank = jnp.dot(lower.astype(BF16), hit.astype(BF16), preferred_element_type=F32)
    sel = jnp.where((rank == lax.rem(lane, blk).astype(F32)), hit, 0.0)
    st[...] = sel
    pick = sel.T.astype(BF16)

    mlane = lax.broadcasted_iota(jnp.int32, (rows, META), 1)
    g_hi = gate.astype(BF16).astype(F32)
    g_mid = (gate - g_hi).astype(BF16).astype(F32)
    g_lo = gate - g_hi - g_mid
    meta = jnp.full((rows, META), -1.0, F32)
    for j in range(top):
        meta = jnp.where(mlane == j, idx[:, j:j + 1].astype(F32), meta)
        meta = jnp.where(mlane == 8 + j, g_hi[:, j:j + 1], meta)
        meta = jnp.where(mlane == 16 + j, g_mid[:, j:j + 1], meta)
        meta = jnp.where(mlane == 24 + j, g_lo[:, j:j + 1], meta)
    sent_meta = jnp.dot(pick, meta.astype(BF16), preferred_element_type=F32).astype(BF16)
    sent = jnp.dot(pick, x_ref[...], preferred_element_type=F32).astype(BF16)
    xr[:blk, :width] = sent[:blk]
    xr[:blk, width:] = sent_meta[:blk]
    send[:, :width] = sent
    send[:, width:] = sent_meta

    pl.semaphore_wait(barrier, n_ep + 1)

    def to_pos(k):
        return remote(send.at[pl.ds(k * blk, blk)], xr.at[place(k, 0)], xs.at[k], xv.at[k], dest(k))

    def spread(k):
        own = xr.at[place(k, 0)]
        return (remote(own, xr.at[place(k, 3)], ys.at[k, 0], yv.at[k, 0], up),
                remote(own, xr.at[place(k, 1)], ys.at[k, 1], yv.at[k, 1], dn))

    def forward(k):
        if k % kl_n < via:
            return remote(xr.at[place(k, 3)], xr.at[place(k, 2)], fs.at[k], fv.at[k], up)
        return remote(xr.at[place(k, 1)], xr.at[place(k, 2)], fs.at[k], fv.at[k], dn)

    def start_spread(k):
        if k:
            to_pos(k).wait_recv()
        for c in spread(k):
            c.start()

    def start_forward(k):
        spread(k)[0 if k % kl_n < via else 1].wait_recv()
        forward(k).start()

    start_spread(0)
    for k in range(1, n_ep):
        to_pos(k).start()
    for k in range(1, kl_n):
        start_spread(k)
        start_forward(k - 1)
    start_forward(kl_n - 1)
    for k in range(kl_n, n_ep):
        start_spread(k)

    half = via * blk

    def opposite(c, n):
        return (remote(part.at[c, n, pl.ds(2 * vrows, half)], near.at[c, n, 0], ns.at[c, n, 0], nv.at[c, n, 0], up),
                remote(part.at[c, n, pl.ds(2 * vrows + half, vrows - half)], near.at[c, n, 1], ns.at[c, n, 1], nv.at[c, n, 1], dn))

    def beside(c, n):
        return (remote(part.at[c, n, pl.ds(vrows, vrows)], full.at[c, n, 0], us.at[c, n, 0], uv.at[c, n, 0], up),
                remote(part.at[c, n, pl.ds(3 * vrows, vrows)], full.at[c, n, 1], us.at[c, n, 1], uv.at[c, n, 1], dn))

    def homeward(k, n):
        return remote(part.at[k // kl_n, n, pl.ds((k % kl_n) * blk, blk)], back.at[n, pl.ds(k * blk, blk)],
                      bs.at[k, n], bv.at[k, n], home(k))

    def start_beside(c, n):
        for r in opposite(c, n):
            r.wait_recv()
        part[c, n, pl.ds(vrows, half)] += near[c, n, 0]
        part[c, n, pl.ds(3 * vrows + half, vrows - half)] += near[c, n, 1]
        for r in beside(c, n):
            r.start()

    def start_homeward(c, n):
        for r in beside(c, n):
            r.wait_recv()
        total = part[c, n, pl.ds(0, vrows)] + full[c, n, 0] + full[c, n, 1]
        part[c, n, pl.ds(0, vrows)] = total
        if c == 0:
            back[n, pl.ds(0, blk)] = total[:blk]
        for k in range(max(c * kl_n, 1), (c + 1) * kl_n):
            homeward(k, n).start()

    for c in range(2):
        for k in range(c * kl_n, (c + 1) * kl_n):
            spread(k)[1 if k % kl_n < via else 0].wait_recv()
            forward(k).wait_recv()

        base = c * crows
        m = xr[pl.ds(base, crows), width:].astype(F32)
        g_sum = m + pltpu.roll(m, META - 8, 1) + pltpu.roll(m, META - 16, 1)
        el = (lax.broadcasted_iota(jnp.int32, (crows, META), 1) + p * n_exp).astype(F32)
        g = jnp.zeros((crows, META), F32)
        for j in range(top):
            g = g + jnp.where(m[:, j:j + 1] == el, g_sum[:, 8 + j:9 + j], 0.0)
        gat[...] = g

        def hidden(e, carry, c=c, base=base):
            if c == 0:
                for w in weights(e)[:2]:
                    w.wait()
                for kl in range(kl_n):
                    @pl.when(e == n_exp - kl_n + kl)
                    def _():
                        start_forward(kl_n + kl)
            else:
                for n in range(n_col):
                    @pl.when(e == n_exp - 2 * n_col + 2 * n + 1)
                    def _():
                        start_beside(0, n)
            xc = xr[pl.ds(base, crows), :width]
            a = jnp.dot(xc, w1[e], preferred_element_type=F32)
            b = jnp.dot(xc, w3[e], preferred_element_type=F32)
            hid[e] = (a * jax.nn.sigmoid(a) * b).astype(BF16)
            return carry

        lax.fori_loop(0, n_exp, hidden, 0)
        if c == 0:
            for e in range(n_exp):
                weights(e)[2].wait()

        def outputs(n, carry, c=c):
            acc = None
            cols = pl.ds(pl.multiple_of(n * COLS, COLS), COLS)
            for e in range(n_exp):
                o = jnp.dot(hid[e], w2[e, :, cols], preferred_element_type=F32) * gat[:, e:e + 1]
                acc = o if acc is None else acc + o
            part[c, n] = acc
            for r in opposite(c, n):
                r.start()
            if c == 1:
                start_homeward(0, n)
            return carry

        lax.fori_loop(0, n_col, outputs, 0)

    for n in range(n_col):
        start_beside(1, n)
    for n in range(n_col):
        start_homeward(1, n)
    for n in range(n_col):
        for k in range(1, n_ep):
            homeward(k, n).wait_recv()
        y_ref[:, n * COLS:(n + 1) * COLS] = jnp.dot(
            st[...], back[n], precision=lax.Precision.HIGHEST, preferred_element_type=F32).astype(BF16)

    for k in range(n_ep):
        if k:
            to_pos(k).wait_send()
        for c in spread(k):
            c.wait_send()
        forward(k).wait_send()
        if k:
            for n in range(n_col):
                homeward(k, n).wait_send()
    for c in range(2):
        for n in range(n_col):
            for r in opposite(c, n) + beside(c, n):
                r.wait_send()


def solution(mesh):
    n_ep = mesh.shape['ep']
    rows_spec = P(('dp', 'ep', 'tp'), None)

    def body(x, idx, gate, w1, w3, w2):
        rows, width = x.shape
        n_exp, _, ff = w1.shape
        blk = 2 * rows // n_ep
        kl_n = n_ep // 2
        vrows, crows, n_col = kl_n * blk, 4 * kl_n * blk, width // COLS
        half = kl_n // 2 * blk
        dma = pltpu.SemaphoreType.DMA
        vmem = pl.BlockSpec(memory_space=pltpu.VMEM)
        anyw = pl.BlockSpec(memory_space=pl.ANY)
        return pl.pallas_call(
            functools.partial(_kernel, n_ep),
            out_shape=jax.ShapeDtypeStruct((rows, width), BF16),
            in_specs=[vmem] * 3 + [anyw] * 3,
            out_specs=vmem,
            scratch_shapes=[
                pltpu.VMEM((rows, n_ep * blk), F32),
                pltpu.VMEM((n_ep * blk, width + META), BF16),
                pltpu.VMEM((2 * crows, width + META), BF16),
                pltpu.VMEM(w1.shape, BF16),
                pltpu.VMEM(w3.shape, BF16),
                pltpu.VMEM(w2.shape, BF16),
                pltpu.VMEM((n_exp, crows, ff), BF16),
                pltpu.VMEM((crows, META), F32),
                pltpu.VMEM((2, n_col, crows, COLS), F32),
                pltpu.VMEM((2, n_col, 2, half, COLS), F32),
                pltpu.VMEM((2, n_col, 2, vrows, COLS), F32),
                pltpu.VMEM((n_col, n_ep * blk, COLS), F32),
                dma((3, n_exp)),
                dma((n_ep,)), dma((n_ep,)),
                dma((n_ep, 2)), dma((n_ep, 2)),
                dma((n_ep,)), dma((n_ep,)),
                dma((2, n_col, 2)), dma((2, n_col, 2)),
                dma((2, n_col, 2)), dma((2, n_col, 2)),
                dma((n_ep, n_col)), dma((n_ep, n_col)),
            ],
            compiler_params=pltpu.CompilerParams(
                collective_id=0, has_side_effects=True, vmem_limit_bytes=63 * 1024 * 1024),
        )(x, idx, gate, w1, w3, w2)

    return jax.shard_map(body, mesh=mesh,
                         in_specs=(rows_spec, rows_spec, rows_spec,
                                   P('ep', None, 'tp'), P('ep', None, 'tp'), P('ep', 'tp', None)),
                         out_specs=rows_spec, check_vma=False)
```

time: 400 us -> 114 us (0.28)
  other arithmetic: 142 us -> 0 us
  waiting for transfers between devices: 111 us -> 0 us
  Pallas kernels: 0 us -> 77.3 us
  blocking collectives: 65.6 us -> 0 us
  matrix products: 26.4 us -> 0 us
  between operations: 14 us -> 0.01 us
    scatter-add x2 -> x0, other arithmetic: 131 us -> none  [the longest x1 97.2 us: _groups(): counts = jnp.zeros((n_exp + 1,), jnp.int32).at[key].add(1)[:n_exp]]
    reduce_scatter x1 -> x0, waiting for transfers between devices: 110 us -> none  [body(): y = lax.psum_scatter(part, ('ep', 'tp'), scatter_dimension=0, tiled=True)]
    pallas_call x0 -> x1, Pallas kernels: none -> 77.3 us  [body(): pl.pallas_call(functools.partial(_kernel, n_ep), out_shape=jax.ShapeDtype...]
    all_gather x2 -> x0, blocking collectives: 65.6 us -> none  [the longest x1 33.1 us: body(): ga = lax.all_gather(gate, ('ep', 'tp'), axis=0, tiled=True)]
    gather x5 -> x0, local copies, waits for them, and re-layouts: 36.5 us -> none  [the longest x1 18.8 us: _experts(): xg = x[tok]]
    unnamed x0 -> x5, local copies, waits for them, and re-layouts: none -> 35.9 us
    dot_general x2 -> x0, matrix products: 26.4 us -> none  [the longest x1 16.1 us: _experts(): jnp.einsum('ecf,efd->ecd', h, w2, preferred_element_type=jnp.float32)]
    sort x1 -> x0, other arithmetic: 8.2 us -> none  [_groups(): order = jnp.argsort(key)]
  transfers between devices with their start and end apart: 2 -> 0, of which waited for: 1 -> 0; matrix products, arithmetic and copies ran while one was open for 32% -> 0% of each run, Pallas kernels for 0% -> 0%
where the time goes in v1:
time: 114 us; the launch traced here: 113 us
  Pallas kernels  77.3 us (68%)
  local copies, waits for them, and re-layouts  35.9 us (31%)
    pallas_call x1, Pallas kernels, body(): pl.pallas_call(functools.partial(_kernel, n_ep), out_shape=jax.ShapeDtype...  77.3 us
    unnamed x5, local copies, waits for them, and re-layouts  35.9 us

profile of v1, /device:TPU:97, one launch (start us, length us, event | category | flops | bytes accessed | tf_op | source)
XLA Modules:
  0.0 113.3 jit_solution(5274120392795251919)
XLA Ops:
  0.0 1.4 %copy.7.idx_ref = s32[64,6]{1,0:T(8,128)} copy(s32[64,6]{0,1:T(8,128)} %param.7) | data formatting | bytes 3072 | tf_op args[1]
  1.4 1.4 %copy.8.gate_ref = f32[64,6]{1,0:T(8,128)} copy(f32[64,6]{0,1:T(8,128)} %param.8) | data formatting | bytes 3072 | tf_op args[2]
  2.8 16.2 %copy.9.w1_hbm = bf16[8,2048,352]{2,1,0:T(8,128)(2,1)} copy(bf16[8,2048,352]{1,2,0:T(8,128)(2,1)} %param.9) | data formatting | bytes 23068672 | tf_op args[3]
  19.0 15.2 %copy.10.w3_hbm = bf16[8,2048,352]{2,1,0:T(8,128)(2,1)} copy(bf16[8,2048,352]{1,2,0:T(8,128)(2,1)} %param.10) | data formatting | bytes 23068672 | tf_op args[4]
  34.3 77.3 %shard_map.64 = bf16[64,2048]{1,0:T(8,128)(2,1)} custom-call(bf16[64,2048]{1,0:T(8,128)(2,1)} %x_ref.1, s32[64,6]{1,0:T(8,128)} %copy.7.idx_ref, f32[64,6]{1,0:T(8,128)} %copy.8.gate_ref, bf16[8,2048,352]{2,1,0:T(8,128)(2,1)} %copy.9.w1_hbm, bf16[8,2048,352]{2,1,0:T(8,128)(2,1)} %copy.10.w3_hbm, bf16[8,352,2048]{2,1,0:T(8,128)(2,1)} %w2_hbm.1), custom_call_target="tpu_custom_call" | custom-call | tf_op jit(solution)/shard_map/pallas_call | solution.py:257
  111.6 1.7 %copy.12 = bf16[64,2048]{1,0:T(8,128)(2,1)} copy(bf16[64,2048]{1,0:T(8,128)(2,1)} %shard_map.64) | data formatting | bytes 524288

commit v2 on v1

--- a/solution.py
+++ b/solution.py
@@ -14,11 +14,14 @@
 
 
 def _kernel(n_ep, x_ref, idx_ref, gate_ref, w1_hbm, w3_hbm, w2_hbm, y_ref,
-            st, send, xr, w1, w3, w2, hid, gat, part, near, full, back,
+            st, mt, send, xr, w13, w2, hid, gat, part, near, full, back,
             w_sem, xs, xv, ys, yv, fs, fv, ns, nv, us, uv, bs, bv):
     rows, width = x_ref.shape
-    top = idx_ref.shape[1]
-    n_exp = w1.shape[0]
+    top = idx_ref.shape[0]
+    n_exp, ff, _ = w2.shape
+    main = ff // 256 * 256
+    rest = -(-(ff - main) // 128) * 128
+    pad = main + rest - ff
     blk = 2 * rows // n_ep
     half_ep = n_ep // 2
     kl_n = n_ep // 2
@@ -44,15 +47,24 @@
         return pltpu.make_async_remote_copy(src_ref=src, dst_ref=dst, send_sem=s, recv_sem=r,
                                             device_id=dev, device_id_type=MESH)
 
-    def weights(e):
-        return [pltpu.make_async_copy(h.at[e], v.at[e], w_sem.at[i, e])
-                for i, (h, v) in enumerate(((w1_hbm, w1), (w3_hbm, w3), (w2_hbm, w2)))]
+    def up_weights(e):
+        parts = []
+        for i, h in enumerate((w1_hbm, w3_hbm)):
+            if main:
+                parts.append((h.at[e, pl.ds(0, main)], w13.at[e, pl.ds(i * main, main)], w_sem.at[2 * i, e]))
+            if rest:
+                parts.append((h.at[e, pl.ds(main, ff - main)], w13.at[e, pl.ds(2 * main + i * rest, ff - main)],
+                              w_sem.at[2 * i + 1, e]))
+        return [pltpu.make_async_copy(*q) for q in parts]
+
+    def down_weights(e):
+        return pltpu.make_async_copy(w2_hbm.at[e], w2.at[e], w_sem.at[4, e])
 
     for e in range(n_exp):
-        for c in weights(e)[:2]:
+        for c in up_weights(e):
             c.start()
     for e in range(n_exp):
-        weights(e)[2].start()
+        down_weights(e).start()
 
     barrier = pltpu.get_barrier_semaphore()
     for k in range(1, n_ep):
@@ -63,32 +75,29 @@
     idx = idx_ref[...]
     gate = gate_ref[...]
     lanes = n_ep * blk
-    lane = lax.broadcasted_iota(jnp.int32, (rows, lanes), 1)
-    kk = lax.div(lane, blk)
+    slot = lax.broadcasted_iota(jnp.int32, (lanes, rows), 0)
+    kk = lax.div(slot, blk)
     pos_of = 2 * lax.rem(cx + half_ep - lax.div(kk, 2), half_ep) + lax.rem(cc + lax.rem(kk, 2), 2)
     first = pos_of * n_exp
-    hit = jnp.zeros((rows, lanes), F32)
+    hit = jnp.zeros((lanes, rows), F32)
     for j in range(top):
-        col = idx[:, j:j + 1]
-        hit = jnp.where((col >= first) & (col < first + n_exp), 1.0, hit)
-    lower = jnp.where(lax.broadcasted_iota(jnp.int32, (rows, rows), 0) > lax.broadcasted_iota(jnp.int32, (rows, rows), 1),
-                      1.0, 0.0)
-    rank = jnp.dot(lower.astype(BF16), hit.astype(BF16), preferred_element_type=F32)
-    sel = jnp.where((rank == lax.rem(lane, blk).astype(F32)), hit, 0.0)
-    st[...] = sel
-    pick = sel.T.astype(BF16)
-
-    mlane = lax.broadcasted_iota(jnp.int32, (rows, META), 1)
+        row = idx[j:j + 1]
+        hit = jnp.where((row >= first) & (row < first + n_exp), 1.0, hit)
+    before = jnp.where(lax.broadcasted_iota(jnp.int32, (rows, rows), 0) < lax.broadcasted_iota(jnp.int32, (rows, rows), 1),
+                       1.0, 0.0)
+    rank = jnp.dot(hit.astype(BF16), before.astype(BF16), preferred_element_type=F32)
+    sel = jnp.where(rank == lax.rem(slot, blk).astype(F32), hit, 0.0)
+    pick = sel.astype(BF16)
+
     g_hi = gate.astype(BF16).astype(F32)
     g_mid = (gate - g_hi).astype(BF16).astype(F32)
-    g_lo = gate - g_hi - g_mid
-    meta = jnp.full((rows, META), -1.0, F32)
-    for j in range(top):
-        meta = jnp.where(mlane == j, idx[:, j:j + 1].astype(F32), meta)
-        meta = jnp.where(mlane == 8 + j, g_hi[:, j:j + 1], meta)
-        meta = jnp.where(mlane == 16 + j, g_mid[:, j:j + 1], meta)
-        meta = jnp.where(mlane == 24 + j, g_lo[:, j:j + 1], meta)
-    sent_meta = jnp.dot(pick, meta.astype(BF16), preferred_element_type=F32).astype(BF16)
+    mt[...] = jnp.zeros_like(mt)
+    mt[0:top] = idx.astype(F32)
+    mt[8:8 + top] = g_hi
+    mt[16:16 + top] = g_mid
+    mt[24:24 + top] = gate - g_hi - g_mid
+    sent_meta = lax.dot_general(pick, mt[...].astype(BF16), (((1,), (1,)), ((), ())),
+                                preferred_element_type=F32).astype(BF16)
     sent = jnp.dot(pick, x_ref[...], preferred_element_type=F32).astype(BF16)
     xr[:blk, :width] = sent[:blk]
     xr[:blk, width:] = sent_meta[:blk]
@@ -100,24 +109,23 @@
     def to_pos(k):
         return remote(send.at[pl.ds(k * blk, blk)], xr.at[place(k, 0)], xs.at[k], xv.at[k], dest(k))
 
-    def spread(k):
-        own = xr.at[place(k, 0)]
-        return (remote(own, xr.at[place(k, 3)], ys.at[k, 0], yv.at[k, 0], up),
-                remote(own, xr.at[place(k, 1)], ys.at[k, 1], yv.at[k, 1], dn))
+    def spread(k, i):
+        return remote(xr.at[place(k, 0)], xr.at[place(k, 1 if i else 3)], ys.at[k, i], yv.at[k, i], dn if i else up)
+
+    def way(k):
+        return 0 if k % kl_n < via else 1
 
     def forward(k):
-        if k % kl_n < via:
-            return remote(xr.at[place(k, 3)], xr.at[place(k, 2)], fs.at[k], fv.at[k], up)
-        return remote(xr.at[place(k, 1)], xr.at[place(k, 2)], fs.at[k], fv.at[k], dn)
+        return remote(xr.at[place(k, 1 if way(k) else 3)], xr.at[place(k, 2)], fs.at[k], fv.at[k], dn if way(k) else up)
 
     def start_spread(k):
         if k:
             to_pos(k).wait_recv()
-        for c in spread(k):
-            c.start()
+        spread(k, 0).start()
+        spread(k, 1).start()
 
     def start_forward(k):
-        spread(k)[0 if k % kl_n < via else 1].wait_recv()
+        spread(k, way(k)).wait_recv()
         forward(k).start()
 
     start_spread(0)
@@ -129,6 +137,10 @@
     start_forward(kl_n - 1)
     for k in range(kl_n, n_ep):
         start_spread(k)
+    st[...] = sel.T
+    if pad:
+        for i in range(2):
+            w13[:, pl.ds(2 * main + i * rest + rest - pad, pad)] = jnp.zeros((n_exp, pad, width), BF16)
 
     half = via * blk
 
@@ -164,7 +176,7 @@
 
     for c in range(2):
         for k in range(c * kl_n, (c + 1) * kl_n):
-            spread(k)[1 if k % kl_n < via else 0].wait_recv()
+            spread(k, 1 - way(k)).wait_recv()
             forward(k).wait_recv()
 
         base = c * crows
@@ -178,7 +190,7 @@
 
         def hidden(e, carry, c=c, base=base):
             if c == 0:
-                for w in weights(e)[:2]:
+                for w in up_weights(e):
                     w.wait()
                 for kl in range(kl_n):
                     @pl.when(e == n_exp - kl_n + kl)
@@ -190,21 +202,23 @@
                     def _():
                         start_beside(0, n)
             xc = xr[pl.ds(base, crows), :width]
-            a = jnp.dot(xc, w1[e], preferred_element_type=F32)
-            b = jnp.dot(xc, w3[e], preferred_element_type=F32)
-            hid[e] = (a * jax.nn.sigmoid(a) * b).astype(BF16)
+            ab = lax.dot_general(xc, w13[e], (((1,), (1,)), ((), ())), preferred_element_type=F32)
+            for at, n in ((0, main), (2 * main, rest)):
+                if n:
+                    a, b = ab[:, at:at + n], ab[:, at + n:at + 2 * n]
+                    hid[e, :, at // 2:at // 2 + n] = (a * jax.nn.sigmoid(a) * b).astype(BF16)
             return carry
 
         lax.fori_loop(0, n_exp, hidden, 0)
         if c == 0:
             for e in range(n_exp):
-                weights(e)[2].wait()
+                down_weights(e).wait()
 
         def outputs(n, carry, c=c):
             acc = None
             cols = pl.ds(pl.multiple_of(n * COLS, COLS), COLS)
             for e in range(n_exp):
-                o = jnp.dot(hid[e], w2[e, :, cols], preferred_element_type=F32) * gat[:, e:e + 1]
+                o = jnp.dot(hid[e, :, :ff], w2[e, :, cols], preferred_element_type=F32) * gat[:, e:e + 1]
                 acc = o if acc is None else acc + o
             part[c, n] = acc
             for r in opposite(c, n):
@@ -228,8 +242,8 @@
     for k in range(n_ep):
         if k:
             to_pos(k).wait_send()
-        for c in spread(k):
-            c.wait_send()
+        spread(k, 0).wait_send()
+        spread(k, 1).wait_send()
         forward(k).wait_send()
         if k:
             for n in range(n_col):
@@ -247,6 +261,7 @@
     def body(x, idx, gate, w1, w3, w2):
         rows, width = x.shape
         n_exp, _, ff = w1.shape
+        wide = ff // 256 * 256 - (-(ff % 256) // 128) * 128
         blk = 2 * rows // n_ep
         kl_n = n_ep // 2
         vrows, crows, n_col = kl_n * blk, 4 * kl_n * blk, width // COLS
@@ -261,18 +276,18 @@
             out_specs=vmem,
             scratch_shapes=[
                 pltpu.VMEM((rows, n_ep * blk), F32),
+                pltpu.VMEM((META, rows), F32),
                 pltpu.VMEM((n_ep * blk, width + META), BF16),
                 pltpu.VMEM((2 * crows, width + META), BF16),
-                pltpu.VMEM(w1.shape, BF16),
-                pltpu.VMEM(w3.shape, BF16),
+                pltpu.VMEM((n_exp, 2 * wide, width), BF16),
                 pltpu.VMEM(w2.shape, BF16),
-                pltpu.VMEM((n_exp, crows, ff), BF16),
+                pltpu.VMEM((n_exp, crows, wide), BF16),
                 pltpu.VMEM((crows, META), F32),
                 pltpu.VMEM((2, n_col, crows, COLS), F32),
                 pltpu.VMEM((2, n_col, 2, half, COLS), F32),
                 pltpu.VMEM((2, n_col, 2, vrows, COLS), F32),
                 pltpu.VMEM((n_col, n_ep * blk, COLS), F32),
-                dma((3, n_exp)),
+                dma((5, n_exp)),
                 dma((n_ep,)), dma((n_ep,)),
                 dma((n_ep, 2)), dma((n_ep, 2)),
                 dma((n_ep,)), dma((n_ep,)),
@@ -282,7 +297,7 @@
             ],
             compiler_params=pltpu.CompilerParams(
                 collective_id=0, has_side_effects=True, vmem_limit_bytes=63 * 1024 * 1024),
-        )(x, idx, gate, w1, w3, w2)
+        )(x, idx.T, gate.T, w1.swapaxes(1, 2), w3.swapaxes(1, 2), w2)
 
     return jax.shard_map(body, mesh=mesh,
                          in_specs=(rows_spec, rows_spec, rows_spec,

time: 114 us -> 76.9 us (0.67)
  local copies, waits for them, and re-layouts: 35.9 us -> 1.67 us
  Pallas kernels: 77.3 us -> 75.1 us
    unnamed x5 -> x1, local copies, waits for them, and re-layouts: 35.9 us -> 1.67 us
    pallas_call x1, Pallas kernels: 77.3 us -> 75.1 us  [body(): pl.pallas_call(functools.partial(_kernel, n_ep), out_shape=jax.ShapeDtype...]
where the time goes in v2:
time: 76.9 us; the launch traced here: 76.8 us
  Pallas kernels  75.1 us (98%)
  local copies, waits for them, and re-layouts  1.67 us (2%)
    pallas_call x1, Pallas kernels, body(): pl.pallas_call(functools.partial(_kernel, n_ep), out_shape=jax.ShapeDtype...  75.1 us
    unnamed x1, local copies, waits for them, and re-layouts  1.67 us

profile of v2, /device:TPU:97, one launch (start us, length us, event | category | flops | bytes accessed | tf_op | source)
XLA Modules:
  0.0 76.8 jit_solution(2340849286899895713)
XLA Ops:
  0.0 75.1 %shard_map.64 = bf16[64,2048]{1,0:T(8,128)(2,1)} custom-call(bf16[64,2048]{1,0:T(8,128)(2,1)} %x_ref.1, s32[6,64]{1,0:T(8,128)} %bitcast.6, f32[6,64]{1,0:T(8,128)} %bitcast.7, bf16[8,352,2048]{2,1,0:T(8,128)(2,1)} %bitcast.4, bf16[8,352,2048]{2,1,0:T(8,128)(2,1)} %bitcast.5, bf16[8,352,2048]{2,1,0:T(8,128)(2,1)} %w2_hbm.1), custom_call_target="tpu_custom_call" | custom-call | tf_op jit(solution)/shard_map/pallas_call | solution.py:272
  75.1 1.7 %copy.8 = bf16[64,2048]{1,0:T(8,128)(2,1)} copy(bf16[64,2048]{1,0:T(8,128)(2,1)} %shard_map.64) | data formatting | bytes 524288

commit v3 on v2

--- a/solution.py
+++ b/solution.py
@@ -8,13 +8,32 @@
 from jax.sharding import PartitionSpec as P
 
 MESH = pl.DeviceIdType.MESH
-F32, BF16 = jnp.float32, jnp.bfloat16
+F32, BF16, I16 = jnp.float32, jnp.bfloat16, jnp.int16
 META = 128
 COLS = 512
+STEPS = 32767.0
+ROUND = 12582912.0
+
+
+def _column(row, n):
+    return jnp.broadcast_to(row, (128, n)).T[:, :1]
+
+
+def _encode(val):
+    n = val.shape[0]
+    top = jnp.maximum(jnp.max(jnp.abs(val), axis=1, keepdims=True), 1e-33)
+    code = (val * (STEPS / top) + ROUND) - ROUND
+    step = jnp.broadcast_to(top * (1.0 / STEPS), (n, 128)).T[:1]
+    return code.astype(jnp.int32).astype(jnp.int16), step
+
+
+def _decode(code, step):
+    return code.astype(jnp.int32).astype(F32) * _column(step, code.shape[0])
 
 
 def _kernel(n_ep, x_ref, idx_ref, gate_ref, w1_hbm, w3_hbm, w2_hbm, y_ref,
-            st, mt, send, xr, w13, w2, hid, gat, part, near, full, back,
+            st, mt, send, xr, w13, w2, hid, gat, part, back, back_s,
+            far_o, far_os, near, near_s, side_o, side_os, full, full_s, home_o, home_os,
             w_sem, xs, xv, ys, yv, fs, fv, ns, nv, us, uv, bs, bv):
     rows, width = x_ref.shape
     top = idx_ref.shape[0]
@@ -34,11 +53,14 @@
     cx, cc = p // 2, p % 2
     up, dn = {'tp': (t + 1) % 4}, {'tp': (t + 3) % 4}
 
+    def away(q):
+        return q if q < 2 else half_ep + 1 - q
+
     def dest(k):
-        return {'ep': 2 * ((cx + half_ep - k // 2) % half_ep) + (cc + k % 2) % 2}
+        return {'ep': 2 * ((cx + half_ep - away(k // 2)) % half_ep) + (cc + k % 2) % 2}
 
     def home(k):
-        return {'ep': 2 * ((cx + k // 2) % half_ep) + (cc + k % 2) % 2}
+        return {'ep': 2 * ((cx + away(k // 2)) % half_ep) + (cc + k % 2) % 2}
 
     def place(k, v):
         return pl.ds((k // kl_n) * crows + v * vrows + (k % kl_n) * blk, blk)
@@ -77,7 +99,8 @@
     lanes = n_ep * blk
     slot = lax.broadcasted_iota(jnp.int32, (lanes, rows), 0)
     kk = lax.div(slot, blk)
-    pos_of = 2 * lax.rem(cx + half_ep - lax.div(kk, 2), half_ep) + lax.rem(cc + lax.rem(kk, 2), 2)
+    q = lax.div(kk, 2)
+    pos_of = 2 * lax.rem(cx + half_ep - jnp.where(q < 2, q, half_ep + 1 - q), half_ep) + lax.rem(cc + lax.rem(kk, 2), 2)
     first = pos_of * n_exp
     hit = jnp.zeros((lanes, rows), F32)
     for j in range(top):
@@ -135,8 +158,6 @@
         start_spread(k)
         start_forward(k - 1)
     start_forward(kl_n - 1)
-    for k in range(kl_n, n_ep):
-        start_spread(k)
     st[...] = sel.T
     if pad:
         for i in range(2):
@@ -145,34 +166,63 @@
     half = via * blk
 
     def opposite(c, n):
-        return (remote(part.at[c, n, pl.ds(2 * vrows, half)], near.at[c, n, 0], ns.at[c, n, 0], nv.at[c, n, 0], up),
-                remote(part.at[c, n, pl.ds(2 * vrows + half, vrows - half)], near.at[c, n, 1], ns.at[c, n, 1], nv.at[c, n, 1], dn))
+        out = []
+        for i, rows_i, dev in ((0, pl.ds(0, half), up), (1, pl.ds(half, vrows - half), dn)):
+            out.append(remote(far_o.at[c, n, rows_i], near.at[c, n, i], ns.at[c, n, i, 0], nv.at[c, n, i, 0], dev))
+            out.append(remote(far_os.at[c, n], near_s.at[c, n, i], ns.at[c, n, i, 1], nv.at[c, n, i, 1], dev))
+        return out
 
     def beside(c, n):
-        return (remote(part.at[c, n, pl.ds(vrows, vrows)], full.at[c, n, 0], us.at[c, n, 0], uv.at[c, n, 0], up),
-                remote(part.at[c, n, pl.ds(3 * vrows, vrows)], full.at[c, n, 1], us.at[c, n, 1], uv.at[c, n, 1], dn))
+        out = []
+        for i, dev in ((0, up), (1, dn)):
+            out.append(remote(side_o.at[c, n, i], full.at[c, n, i], us.at[c, n, i, 0], uv.at[c, n, i, 0], dev))
+            out.append(remote(side_os.at[c, n, i], full_s.at[c, n, i], us.at[c, n, i, 1], uv.at[c, n, i, 1], dev))
+        return out
 
     def homeward(k, n):
-        return remote(part.at[k // kl_n, n, pl.ds((k % kl_n) * blk, blk)], back.at[n, pl.ds(k * blk, blk)],
-                      bs.at[k, n], bv.at[k, n], home(k))
+        c = k // kl_n
+        return [remote(home_o.at[c, n, pl.ds((k % kl_n) * blk, blk)], back.at[n, pl.ds(k * blk, blk)],
+                       bs.at[k, n, 0], bv.at[k, n, 0], home(k)),
+                remote(home_os.at[c, n], back_s.at[n, k], bs.at[k, n, 1], bv.at[k, n, 1], home(k))]
+
+    def start_opposite(c, n):
+        code, step = _encode(part[c, n, pl.ds(2 * vrows, vrows)])
+        far_o[c, n] = code
+        far_os[c, n] = step
+        for r in opposite(c, n):
+            r.start()
 
     def start_beside(c, n):
         for r in opposite(c, n):
             r.wait_recv()
-        part[c, n, pl.ds(vrows, half)] += near[c, n, 0]
-        part[c, n, pl.ds(3 * vrows + half, vrows - half)] += near[c, n, 1]
+        for i, at in ((0, 0), (1, half)):
+            v = (1, 3)[i] * vrows
+            size = vrows - half if i else half
+            step = near_s[c, n, i][:, at:at + size]
+            more = _decode(near[c, n, i], step)
+            mine = part[c, n, pl.ds(v, vrows)]
+            mine = jnp.concatenate([mine[:half], mine[half:] + more] if i else [mine[:half] + more, mine[half:]], axis=0)
+            code, step = _encode(mine)
+            side_o[c, n, i] = code
+            side_os[c, n, i] = step
         for r in beside(c, n):
             r.start()
 
     def start_homeward(c, n):
         for r in beside(c, n):
             r.wait_recv()
-        total = part[c, n, pl.ds(0, vrows)] + full[c, n, 0] + full[c, n, 1]
-        part[c, n, pl.ds(0, vrows)] = total
+        total = part[c, n, pl.ds(0, vrows)]
+        for i in range(2):
+            total = total + _decode(full[c, n, i], full_s[c, n, i])
+        code, step = _encode(total)
+        home_o[c, n] = code
+        home_os[c, n] = step
         if c == 0:
-            back[n, pl.ds(0, blk)] = total[:blk]
+            back[n, pl.ds(0, blk)] = code[:blk]
+            back_s[n, 0] = step
         for k in range(max(c * kl_n, 1), (c + 1) * kl_n):
-            homeward(k, n).start()
+            for r in homeward(k, n):
+                r.start()
 
     for c in range(2):
         for k in range(c * kl_n, (c + 1) * kl_n):
@@ -193,6 +243,10 @@
                 for w in up_weights(e):
                     w.wait()
                 for kl in range(kl_n):
+                    @pl.when(e == n_exp - 2 * kl_n + kl)
+                    def _():
+                        start_spread(kl_n + kl)
+
                     @pl.when(e == n_exp - kl_n + kl)
                     def _():
                         start_forward(kl_n + kl)
@@ -221,23 +275,32 @@
                 o = jnp.dot(hid[e, :, :ff], w2[e, :, cols], preferred_element_type=F32) * gat[:, e:e + 1]
                 acc = o if acc is None else acc + o
             part[c, n] = acc
-            for r in opposite(c, n):
-                r.start()
+            start_opposite(c, n)
             if c == 1:
                 start_homeward(0, n)
+
+                @pl.when(n >= 2)
+                def _():
+                    start_beside(1, n - 2)
             return carry
 
         lax.fori_loop(0, n_col, outputs, 0)
 
-    for n in range(n_col):
+    for n in range(max(n_col - 2, 0), n_col):
         start_beside(1, n)
     for n in range(n_col):
         start_homeward(1, n)
+    lane_k = lax.div(lax.broadcasted_iota(jnp.int32, (1, lanes), 1), blk)
     for n in range(n_col):
-        for k in range(1, n_ep):
-            homeward(k, n).wait_recv()
+        steps = jnp.zeros((1, lanes), F32)
+        for k in range(n_ep):
+            if k:
+                for r in homeward(k, n):
+                    r.wait_recv()
+            row = back_s[n, k]
+            steps = jnp.where(lane_k == k, jnp.concatenate([row] * 2, axis=1), steps)
         y_ref[:, n * COLS:(n + 1) * COLS] = jnp.dot(
-            st[...], back[n], precision=lax.Precision.HIGHEST, preferred_element_type=F32).astype(BF16)
+            st[...], _decode(back[n], steps), precision=lax.Precision.HIGHEST, preferred_element_type=F32).astype(BF16)
 
     for k in range(n_ep):
         if k:
@@ -247,7 +310,8 @@
         forward(k).wait_send()
         if k:
             for n in range(n_col):
-                homeward(k, n).wait_send()
+                for r in homeward(k, n):
+                    r.wait_send()
     for c in range(2):
         for n in range(n_col):
             for r in opposite(c, n) + beside(c, n):
@@ -284,16 +348,25 @@
                 pltpu.VMEM((n_exp, crows, wide), BF16),
                 pltpu.VMEM((crows, META), F32),
                 pltpu.VMEM((2, n_col, crows, COLS), F32),
-                pltpu.VMEM((2, n_col, 2, half, COLS), F32),
-                pltpu.VMEM((2, n_col, 2, vrows, COLS), F32),
-                pltpu.VMEM((n_col, n_ep * blk, COLS), F32),
+                pltpu.VMEM((n_col, n_ep * blk, COLS), I16),
+                pltpu.VMEM((n_col, n_ep, 1, vrows), F32),
+                pltpu.VMEM((2, n_col, vrows, COLS), I16),
+                pltpu.VMEM((2, n_col, 1, vrows), F32),
+                pltpu.VMEM((2, n_col, 2, half, COLS), I16),
+                pltpu.VMEM((2, n_col, 2, 1, vrows), F32),
+                pltpu.VMEM((2, n_col, 2, vrows, COLS), I16),
+                pltpu.VMEM((2, n_col, 2, 1, vrows), F32),
+                pltpu.VMEM((2, n_col, 2, vrows, COLS), I16),
+                pltpu.VMEM((2, n_col, 2, 1, vrows), F32),
+                pltpu.VMEM((2, n_col, vrows, COLS), I16),
+                pltpu.VMEM((2, n_col, 1, vrows), F32),
                 dma((5, n_exp)),
                 dma((n_ep,)), dma((n_ep,)),
                 dma((n_ep, 2)), dma((n_ep, 2)),
                 dma((n_ep,)), dma((n_ep,)),
-                dma((2, n_col, 2)), dma((2, n_col, 2)),
-                dma((2, n_col, 2)), dma((2, n_col, 2)),
-                dma((n_ep, n_col)), dma((n_ep, n_col)),
+                dma((2, n_col, 2, 2)), dma((2, n_col, 2, 2)),
+                dma((2, n_col, 2, 2)), dma((2, n_col, 2, 2)),
+                dma((n_ep, n_col, 2)), dma((n_ep, n_col, 2)),
             ],
             compiler_params=pltpu.CompilerParams(
                 collective_id=0, has_side_effects=True, vmem_limit_bytes=63 * 1024 * 1024),

time: 76.9 us -> 73.1 us (0.951)
  Pallas kernels: 75.1 us -> 71.3 us
    pallas_call x1, Pallas kernels: 75.1 us -> 71.3 us  [body(): pl.pallas_call(functools.partial(_kernel, n_ep), out_shape=jax.ShapeDtype...]
where the time goes in v3:
time: 73.1 us; the launch traced here: 73 us
  Pallas kernels  71.3 us (98%)
  local copies, waits for them, and re-layouts  1.67 us (2%)
    pallas_call x1, Pallas kernels, body(): pl.pallas_call(functools.partial(_kernel, n_ep), out_shape=jax.ShapeDtype...  71.3 us
    unnamed x1, local copies, waits for them, and re-layouts  1.67 us

profile of v3, /device:TPU:97, one launch (start us, length us, event | category | flops | bytes accessed | tf_op | source)
XLA Modules:
  0.0 73.0 jit_solution(12998450408484788636)
XLA Ops:
  0.0 71.3 %shard_map.64 = bf16[64,2048]{1,0:T(8,128)(2,1)} custom-call(bf16[64,2048]{1,0:T(8,128)(2,1)} %x_ref.1, s32[6,64]{1,0:T(8,128)} %bitcast.6, f32[6,64]{1,0:T(8,128)} %bitcast.7, bf16[8,352,2048]{2,1,0:T(8,128)(2,1)} %bitcast.4, bf16[8,352,2048]{2,1,0:T(8,128)(2,1)} %bitcast.5, bf16[8,352,2048]{2,1,0:T(8,128)(2,1)} %w2_hbm.1), custom_call_target="tpu_custom_call" | custom-call | tf_op jit(solution)/shard_map/pallas_call | solution.py:336
  71.3 1.7 %copy.8 = bf16[64,2048]{1,0:T(8,128)(2,1)} copy(bf16[64,2048]{1,0:T(8,128)(2,1)} %shard_map.64) | data formatting | bytes 524288

commit v4 on v3

--- a/solution.py
+++ b/solution.py
@@ -10,20 +10,24 @@
 MESH = pl.DeviceIdType.MESH
 F32, BF16, I16 = jnp.float32, jnp.bfloat16, jnp.int16
 META = 128
-COLS = 512
+COLS = 1024
 STEPS = 32767.0
 ROUND = 12582912.0
 
 
+def _diagonal(n):
+    return lax.broadcasted_iota(jnp.int32, (n, n), 0) == lax.broadcasted_iota(jnp.int32, (n, n), 1)
+
+
 def _column(row, n):
-    return jnp.broadcast_to(row, (128, n)).T[:, :1]
+    return jnp.sum(jnp.where(_diagonal(n), row, 0.0), axis=1, keepdims=True)
 
 
 def _encode(val):
     n = val.shape[0]
     top = jnp.maximum(jnp.max(jnp.abs(val), axis=1, keepdims=True), 1e-33)
     code = (val * (STEPS / top) + ROUND) - ROUND
-    step = jnp.broadcast_to(top * (1.0 / STEPS), (n, 128)).T[:1]
+    step = jnp.sum(jnp.where(_diagonal(n), top * (1.0 / STEPS), 0.0), axis=0, keepdims=True)
     return code.astype(jnp.int32).astype(jnp.int16), step
 
 
@@ -158,6 +162,8 @@
         start_spread(k)
         start_forward(k - 1)
     start_forward(kl_n - 1)
+    for k in range(kl_n, n_ep):
+        start_spread(k)
     st[...] = sel.T
     if pad:
         for i in range(2):
@@ -185,32 +191,26 @@
                        bs.at[k, n, 0], bv.at[k, n, 0], home(k)),
                 remote(home_os.at[c, n], back_s.at[n, k], bs.at[k, n, 1], bv.at[k, n, 1], home(k))]
 
-    def start_opposite(c, n):
-        code, step = _encode(part[c, n, pl.ds(2 * vrows, vrows)])
-        far_o[c, n] = code
-        far_os[c, n] = step
-        for r in opposite(c, n):
+    def wait_all(copies):
+        for r in copies:
+            r.wait_recv()
+
+    def start_all(copies):
+        for r in copies:
             r.start()
 
-    def start_beside(c, n):
-        for r in opposite(c, n):
-            r.wait_recv()
+    def make_opposite(c, n):
+        far_o[c, n], far_os[c, n] = _encode(part[c, n, pl.ds(2 * vrows, vrows)])
+
+    def make_beside(c, n):
         for i, at in ((0, 0), (1, half)):
-            v = (1, 3)[i] * vrows
             size = vrows - half if i else half
-            step = near_s[c, n, i][:, at:at + size]
-            more = _decode(near[c, n, i], step)
-            mine = part[c, n, pl.ds(v, vrows)]
+            more = _decode(near[c, n, i], near_s[c, n, i][:, at:at + size])
+            mine = part[c, n, pl.ds((1, 3)[i] * vrows, vrows)]
             mine = jnp.concatenate([mine[:half], mine[half:] + more] if i else [mine[:half] + more, mine[half:]], axis=0)
-            code, step = _encode(mine)
-            side_o[c, n, i] = code
-            side_os[c, n, i] = step
-        for r in beside(c, n):
-            r.start()
-
-    def start_homeward(c, n):
-        for r in beside(c, n):
-            r.wait_recv()
+            side_o[c, n, i], side_os[c, n, i] = _encode(mine)
+
+    def make_homeward(c, n):
         total = part[c, n, pl.ds(0, vrows)]
         for i in range(2):
             total = total + _decode(full[c, n, i], full_s[c, n, i])
@@ -220,17 +220,16 @@
         if c == 0:
             back[n, pl.ds(0, blk)] = code[:blk]
             back_s[n, 0] = step
+
+    def start_homeward(c, n):
         for k in range(max(c * kl_n, 1), (c + 1) * kl_n):
-            for r in homeward(k, n):
-                r.start()
-
-    for c in range(2):
+            start_all(homeward(k, n))
+
+    def gather(c):
         for k in range(c * kl_n, (c + 1) * kl_n):
             spread(k, 1 - way(k)).wait_recv()
             forward(k).wait_recv()
-
-        base = c * crows
-        m = xr[pl.ds(base, crows), width:].astype(F32)
+        m = xr[pl.ds(c * crows, crows), width:].astype(F32)
         g_sum = m + pltpu.roll(m, META - 8, 1) + pltpu.roll(m, META - 16, 1)
         el = (lax.broadcasted_iota(jnp.int32, (crows, META), 1) + p * n_exp).astype(F32)
         g = jnp.zeros((crows, META), F32)
@@ -238,57 +237,86 @@
             g = g + jnp.where(m[:, j:j + 1] == el, g_sum[:, 8 + j:9 + j], 0.0)
         gat[...] = g
 
-        def hidden(e, carry, c=c, base=base):
-            if c == 0:
-                for w in up_weights(e):
-                    w.wait()
-                for kl in range(kl_n):
-                    @pl.when(e == n_exp - 2 * kl_n + kl)
-                    def _():
-                        start_spread(kl_n + kl)
-
-                    @pl.when(e == n_exp - kl_n + kl)
-                    def _():
-                        start_forward(kl_n + kl)
-            else:
-                for n in range(n_col):
-                    @pl.when(e == n_exp - 2 * n_col + 2 * n + 1)
-                    def _():
-                        start_beside(0, n)
-            xc = xr[pl.ds(base, crows), :width]
-            ab = lax.dot_general(xc, w13[e], (((1,), (1,)), ((), ())), preferred_element_type=F32)
-            for at, n in ((0, main), (2 * main, rest)):
-                if n:
-                    a, b = ab[:, at:at + n], ab[:, at + n:at + 2 * n]
-                    hid[e, :, at // 2:at // 2 + n] = (a * jax.nn.sigmoid(a) * b).astype(BF16)
-            return carry
-
-        lax.fori_loop(0, n_exp, hidden, 0)
-        if c == 0:
-            for e in range(n_exp):
-                down_weights(e).wait()
-
-        def outputs(n, carry, c=c):
-            acc = None
-            cols = pl.ds(pl.multiple_of(n * COLS, COLS), COLS)
-            for e in range(n_exp):
-                o = jnp.dot(hid[e, :, :ff], w2[e, :, cols], preferred_element_type=F32) * gat[:, e:e + 1]
-                acc = o if acc is None else acc + o
-            part[c, n] = acc
-            start_opposite(c, n)
-            if c == 1:
-                start_homeward(0, n)
-
-                @pl.when(n >= 2)
-                def _():
-                    start_beside(1, n - 2)
-            return carry
-
-        lax.fori_loop(0, n_col, outputs, 0)
-
-    for n in range(max(n_col - 2, 0), n_col):
-        start_beside(1, n)
+    def hidden(c, e):
+        ab = lax.dot_general(xr[pl.ds(c * crows, crows), :width], w13[e], (((1,), (1,)), ((), ())),
+                             preferred_element_type=F32)
+        for at, n in ((0, main), (2 * main, rest)):
+            if n:
+                a, b = ab[:, at:at + n], ab[:, at + n:at + 2 * n]
+                hid[e, :, at // 2:at // 2 + n] = (a * jax.nn.sigmoid(a) * b).astype(BF16)
+
+    def outputs(c, n, between):
+        acc = None
+        for e in range(n_exp):
+            if e % 2 and between:
+                between.pop(0)()
+            o = jnp.dot(hid[e, :, :ff], w2[e, :, n * COLS:(n + 1) * COLS], preferred_element_type=F32) * gat[:, e:e + 1]
+            acc = o if acc is None else acc + o
+        for b in between:
+            b()
+        part[c, n] = acc
+
+    gather(0)
+
+    def first(e, carry):
+        for w in up_weights(e):
+            w.wait()
+        for kl in range(kl_n - 1):
+            @pl.when(e == 2 * kl + 2)
+            def _():
+                start_forward(kl_n + kl)
+        hidden(0, e)
+        return carry
+
+    lax.fori_loop(0, n_exp, first, 0)
+    start_forward(n_ep - 1)
+    for e in range(n_exp):
+        down_weights(e).wait()
     for n in range(n_col):
+        outputs(0, n, [])
+        make_opposite(0, n)
+        start_all(opposite(0, n))
+
+    gather(1)
+    each = n_exp // n_col
+
+    def second(n, carry):
+        for i in range(each):
+            if i == each // 2:
+                wait_all(opposite(0, n))
+                make_beside(0, n)
+                start_all(beside(0, n))
+            hidden(1, n * each + i)
+        return carry
+
+    lax.fori_loop(0, n_col, second, 0)
+    last = n_col - 1
+    for n in range(n_col):
+        work = []
+        if n:
+            wait_all(beside(0, n - 1))
+            work.append(lambda: make_homeward(0, n - 1))
+        if n == last and n > 1:
+            wait_all(opposite(1, 0))
+            work.append(lambda: make_beside(1, 0))
+        outputs(1, n, work)
+        make_opposite(1, n)
+        start_all(opposite(1, n))
+        if n == last and n > 1:
+            start_all(beside(1, 0))
+        if n:
+            start_homeward(0, n - 1)
+    for n in range(1 if last > 1 else 0, n_col):
+        if n == last:
+            wait_all(beside(0, last))
+            make_homeward(0, last)
+            start_homeward(0, last)
+        wait_all(opposite(1, n))
+        make_beside(1, n)
+        start_all(beside(1, n))
+    for n in range(n_col):
+        wait_all(beside(1, n))
+        make_homeward(1, n)
         start_homeward(1, n)
     lane_k = lax.div(lax.broadcasted_iota(jnp.int32, (1, lanes), 1), blk)
     for n in range(n_col):

time: 73.1 us -> 68.5 us (0.937)
  Pallas kernels: 71.3 us -> 66.7 us
    pallas_call x1, Pallas kernels: 71.3 us -> 66.7 us  [body(): pl.pallas_call(functools.partial(_kernel, n_ep), out_shape=jax.ShapeDtype...]
where the time goes in v4:
time: 68.5 us; the launch traced here: 68.4 us
  Pallas kernels  66.7 us (97%)
  local copies, waits for them, and re-layouts  1.67 us (2%)
    pallas_call x1, Pallas kernels, body(): pl.pallas_call(functools.partial(_kernel, n_ep), out_shape=jax.ShapeDtype...  66.7 us
    unnamed x1, local copies, waits for them, and re-layouts  1.67 us

profile of v4, /device:TPU:97, one launch (start us, length us, event | category | flops | bytes accessed | tf_op | source)
XLA Modules:
  0.0 68.4 jit_solution(3847482365676672983)
XLA Ops:
  0.0 66.7 %shard_map.64 = bf16[64,2048]{1,0:T(8,128)(2,1)} custom-call(bf16[64,2048]{1,0:T(8,128)(2,1)} %x_ref.1, s32[6,64]{1,0:T(8,128)} %bitcast.6, f32[6,64]{1,0:T(8,128)} %bitcast.7, bf16[8,352,2048]{2,1,0:T(8,128)(2,1)} %bitcast.4, bf16[8,352,2048]{2,1,0:T(8,128)(2,1)} %bitcast.5, bf16[8,352,2048]{2,1,0:T(8,128)(2,1)} %w2_hbm.1), custom_call_target="tpu_custom_call" | custom-call | tf_op jit(solution)/shard_map/pallas_call | solution.py:364
  66.7 1.7 %copy.8 = bf16[64,2048]{1,0:T(8,128)(2,1)} copy(bf16[64,2048]{1,0:T(8,128)(2,1)} %shard_map.64) | data formatting | bytes 524288

commit v5 on v4

--- a/solution.py
+++ b/solution.py
@@ -145,6 +145,16 @@
     def forward(k):
         return remote(xr.at[place(k, 1 if way(k) else 3)], xr.at[place(k, 2)], fs.at[k], fv.at[k], dn if way(k) else up)
 
+    def late(v, lo, hi):
+        return xr.at[pl.ds(crows + v * vrows + lo, hi - lo)]
+
+    def spread_late(i):
+        return remote(late(0, 0, vrows), late(1 if i else 3, 0, vrows), ys.at[kl_n, i], yv.at[kl_n, i], dn if i else up)
+
+    def forward_late(i):
+        lo, hi = (via * blk, vrows) if i else (0, via * blk)
+        return remote(late(1 if i else 3, lo, hi), late(2, lo, hi), fs.at[kl_n + i], fv.at[kl_n + i], dn if i else up)
+
     def start_spread(k):
         if k:
             to_pos(k).wait_recv()
@@ -163,7 +173,9 @@
         start_forward(k - 1)
     start_forward(kl_n - 1)
     for k in range(kl_n, n_ep):
-        start_spread(k)
+        to_pos(k).wait_recv()
+    for i in range(2):
+        spread_late(i).start()
     st[...] = sel.T
     if pad:
         for i in range(2):
@@ -226,9 +238,11 @@
             start_all(homeward(k, n))
 
     def gather(c):
-        for k in range(c * kl_n, (c + 1) * kl_n):
+        for k in range(0 if c else kl_n):
             spread(k, 1 - way(k)).wait_recv()
             forward(k).wait_recv()
+        for i in range(2 if c else 0):
+            forward_late(i).wait_recv()
         m = xr[pl.ds(c * crows, crows), width:].astype(F32)
         g_sum = m + pltpu.roll(m, META - 8, 1) + pltpu.roll(m, META - 16, 1)
         el = (lax.broadcasted_iota(jnp.int32, (crows, META), 1) + p * n_exp).astype(F32)
@@ -261,15 +275,16 @@
     def first(e, carry):
         for w in up_weights(e):
             w.wait()
-        for kl in range(kl_n - 1):
-            @pl.when(e == 2 * kl + 2)
-            def _():
-                start_forward(kl_n + kl)
+        @pl.when(e == n_exp - 3)
+        def _():
+            for i in range(2):
+                spread_late(i).wait_recv()
+                forward_late(i).start()
+
         hidden(0, e)
         return carry
 
     lax.fori_loop(0, n_exp, first, 0)
-    start_forward(n_ep - 1)
     for e in range(n_exp):
         down_weights(e).wait()
     for n in range(n_col):
@@ -333,13 +348,17 @@
     for k in range(n_ep):
         if k:
             to_pos(k).wait_send()
-        spread(k, 0).wait_send()
-        spread(k, 1).wait_send()
-        forward(k).wait_send()
+        if k < kl_n:
+            spread(k, 0).wait_send()
+            spread(k, 1).wait_send()
+            forward(k).wait_send()
         if k:
             for n in range(n_col):
                 for r in homeward(k, n):
                     r.wait_send()
+    for i in range(2):
+        spread_late(i).wait_send()
+        forward_late(i).wait_send()
     for c in range(2):
         for n in range(n_col):
             for r in opposite(c, n) + beside(c, n):

time: 68.5 us -> 68.2 us (level)
  no operation moved by 1% of the time
where the time goes in v5:
time: 68.2 us; the launch traced here: 68.1 us
  Pallas kernels  66.4 us (97%)
  local copies, waits for them, and re-layouts  1.67 us (2%)
    pallas_call x1, Pallas kernels, body(): pl.pallas_call(functools.partial(_kernel, n_ep), out_shape=jax.ShapeDtype...  66.4 us
    unnamed x1, local copies, waits for them, and re-layouts  1.67 us

profile of v5, /device:TPU:97, one launch (start us, length us, event | category | flops | bytes accessed | tf_op | source)
XLA Modules:
  0.0 68.1 jit_solution(1839893327758421631)
XLA Ops:
  0.0 66.4 %shard_map.64 = bf16[64,2048]{1,0:T(8,128)(2,1)} custom-call(bf16[64,2048]{1,0:T(8,128)(2,1)} %x_ref.1, s32[6,64]{1,0:T(8,128)} %bitcast.6, f32[6,64]{1,0:T(8,128)} %bitcast.7, bf16[8,352,2048]{2,1,0:T(8,128)(2,1)} %bitcast.4, bf16[8,352,2048]{2,1,0:T(8,128)(2,1)} %bitcast.5, bf16[8,352,2048]{2,1,0:T(8,128)(2,1)} %w2_hbm.1), custom_call_target="tpu_custom_call" | custom-call | tf_op jit(solution)/shard_map/pallas_call | solution.py:383
  66.4 1.7 %copy.8 = bf16[64,2048]{1,0:T(8,128)(2,1)} copy(bf16[64,2048]{1,0:T(8,128)(2,1)} %shard_map.64) | data formatting | bytes 524288
